TPU v7x, 128 devices: a whole 4x4x4 slice. The times are simulated.
128 devices in a mesh: dp: 8 (over y, core), tensor: 16 (over x, z).
Axes of the slice: x: 4, y: 4, z: 4, core: 2. Of those that a mesh axis runs over, the one named last changes fastest.
Arguments:
- ref_hidden: bfloat16 [2304, 4608], P('dp', 'tensor'), may hold values from -6 to 6
- pol_hidden: bfloat16 [2304, 4608], P('dp', 'tensor'), may hold values from -6 to 6
- readout: bfloat16 [2304, 4608], P('dp', 'tensor'), may hold values from -0.019897461 to 0.019897461
- lengths: int32 [24], P('dp'), may hold values from 16 to 96, as said below
- pairing: int32 [24], replicated, may hold values from 0 to 23, each once
- pre_gain: float32 [4608], replicated, may hold values from 0.25 to 1.75
- post_gain: float32 [4608], replicated, may hold values from 0.25 to 1.75
- w_query: bfloat16 [4608, 4096], P('dp', 'tensor'), may hold values from -0.09375 to 0.09375
- w_key: bfloat16 [4608, 2048], P('dp', 'tensor'), may hold values from -3 to 3
- value_projection: bfloat16 [4608, 2048], P('dp', 'tensor'), may hold values from -0.09375 to 0.09375
- w_out: bfloat16 [4608, 4096], P('dp', 'tensor'), may hold values from -0.09375 to 0.09375
- a_query: bfloat16 [4608, 64], P('dp'), may hold values from -0.09375 to 0.09375
- a_value: bfloat16 [4608, 64], P('dp'), may hold values from -0.09375 to 0.09375
- query_second_factor: bfloat16 [64, 4096], P(None, 'tensor'), may hold values from -0.75 to 0.75
- value_second_factor: bfloat16 [64, 2048], P(None, 'tensor'), may hold values from -0.75 to 0.75
Outputs:
- policy_out: bfloat16 [2304, 4608], P('dp', 'tensor')
- reference_out: bfloat16 [2304, 4608], P('dp', 'tensor')
- dpo_loss: float32 [], replicated
- grad_hidden: bfloat16 [2304, 4608], P('dp', 'tensor')
- grad_a: float32 [4608, 128], P('dp')
- query_factor_gradient: float32 [64, 4096], P(None, 'tensor')
- value_factor_gradient: float32 [64, 2048], P(None, 'tensor')
Inputs may be any that keep to these rules, and one draw needn't show every extreme that they name: `lengths`: every sequence has at least one valid token and some sequence is full. `pairing`: entries 2k and 2k + 1 name the chosen and the rejected sequence of pair k; every sequence appears once.
All inputs are finite; a program needn't handle non-finite values.
Results may differ from a plain program's by a relative error of at most 0.0233.
The roundings to bfloat16 on the way count: a program that leaves them out, or rounds other values in their place, can miss the bound.
Values may be sent and summed in bfloat16 or wider, within the bound.
A program may use at most 128 MiB of HBM per device.

v0:
```python
import functools
import jax
import jax.numpy as jnp
from jax import lax
from jax.sharding import Mesh
from jax.sharding import PartitionSpec as P

MODEL_WIDTH = 4608
HQ = 32
HEAD_SIZE = 128
TENSOR = ("tensor_0", "tensor_1")
DP = ("dp_0", "dp_1")
DP_TENSOR = ("dp_0", "dp_1", "tensor_0", "tensor_1")
NORM_EPS = 1e-06
SOFT_CAP = 50.0
ADAPTER_SCALE = 0.5
DPO_BETA = 0.5
LOSS_SCALE = 256.0
ROPE_BASE = 10000.0


def one_axis_at_a_time(shard, axes):
    return functools.reduce(lax.psum, axes, shard)


def copy_for_each(shard, axis):
    count = lax.axis_size(axis)
    return lax.all_to_all(
        jnp.broadcast_to(shard[None], (count, *shard.shape)), axis, 0, 0, tiled=True
    )


def in_order(tiles, dim):
    shape = list(tiles.shape[1:])
    shape[dim] *= tiles.shape[0]
    return jnp.moveaxis(tiles, 0, dim).reshape(shape)


def collect(shard, axis, dim):
    tiles = copy_for_each(shard, axis)
    return in_order(tiles, dim)


def split_up(shard, dim, count):
    shape = shard.shape
    tiles = shard.reshape(*shape[:dim], count, shape[dim] // count, *shape[dim + 1 :])
    return jnp.moveaxis(tiles, dim, 0)


def summed_on_arrival(shard, axis, dim):
    tiles = split_up(shard, dim, lax.axis_size(axis))
    arrived = lax.all_to_all(tiles, axis, split_axis=0, concat_axis=0, tiled=True)
    return arrived.astype(jnp.float32).sum(axis=0)


def sent_together(arrays, axis, dim, along):
    ends, at = ([], 0)
    for a in arrays[:-1]:
        at += a.shape[along]
        ends.append(at)
    both = jnp.concatenate(arrays, axis=along)
    return tuple(jnp.split(lax.all_gather(both, axis, axis=dim, tiled=True), ends, axis=along))


def over_copies(shard, axis):
    return copy_for_each(shard, axis).astype(jnp.float32).sum(axis=0)


def query_scale():
    return float(MODEL_WIDTH // HQ) ** (-0.5)


def apply_rotation(value_rows, direction):
    length = value_rows.shape[1]
    head_depth = value_rows.shape[3]
    middle = head_depth // 2
    spacing = ROPE_BASE ** (-2.0 * jnp.arange(middle, dtype=jnp.float32) / head_depth)
    angles = jnp.arange(length, dtype=jnp.float32)[:, None] * spacing[None, :]
    cosine = jnp.cos(angles)[None, :, None, :]
    sine_part = direction * jnp.sin(angles)[None, :, None, :]
    leading = value_rows[..., :middle]
    trailing = value_rows[..., middle:]
    return jnp.concatenate(
        [leading * cosine - trailing * sine_part, trailing * cosine + leading * sine_part], axis=-1
    )


def allowed_mask(lengths, length):
    places = jnp.arange(length)
    causal = places[None, :] <= places[:, None]
    living = places[None, :] < lengths[:, None]
    return causal[None, None, None, :, :] & living[:, None, None, None, :]


def attend(query_rows, rotated_keys, value_rows, lengths):
    seqs_here, length, q_heads, head_depth = query_rows.shape
    kv_heads = rotated_keys.shape[2]
    grouped_heads = query_rows.reshape(seqs_here, length, kv_heads, q_heads // kv_heads, head_depth)
    scores = (
        jnp.einsum(
            "sqkgd,spkd->skgqp", grouped_heads, rotated_keys, preferred_element_type=jnp.float32
        )
        * query_scale()
    )
    capped = SOFT_CAP * jnp.tanh(scores / SOFT_CAP)
    allowed = allowed_mask(lengths, length)
    weights = jnp.where(allowed, jnp.exp(capped), 0.0)
    probabilities = weights / jnp.sum(weights, axis=-1, keepdims=True)
    probs_low = probabilities.astype(jnp.bfloat16)
    mixed_out = jnp.einsum(
        "skgqp,spkd->sqkgd", probs_low, value_rows, preferred_element_type=jnp.float32
    )
    return (
        mixed_out.astype(jnp.bfloat16).reshape(seqs_here, length, q_heads, head_depth),
        probs_low,
        probabilities,
        capped,
    )


def attend_back(grad_mixed, query_rows, rotated_keys, value_rows, probs_low, probabilities, capped):
    seqs_here, length, q_heads, head_depth = query_rows.shape
    kv_heads = rotated_keys.shape[2]
    shape_five = (seqs_here, length, kv_heads, q_heads // kv_heads, head_depth)
    grouped_heads = query_rows.reshape(shape_five)
    grad_grouped = grad_mixed.reshape(shape_five)
    grad_probs = jnp.einsum(
        "sqkgd,spkd->skgqp", grad_grouped, value_rows, preferred_element_type=jnp.float32
    )
    value_rows_gradient = jnp.einsum(
        "skgqp,sqkgd->spkd", probs_low, grad_grouped, preferred_element_type=jnp.float32
    )
    centered = grad_probs - jnp.sum(grad_probs * probabilities, axis=-1, keepdims=True)
    grad_scores = (
        probabilities * centered * (1.0 - (capped / SOFT_CAP) ** 2) * query_scale()
    ).astype(jnp.bfloat16)
    query_rows_gradient = jnp.einsum(
        "skgqp,spkd->sqkgd", grad_scores, rotated_keys, preferred_element_type=jnp.float32
    ).reshape(seqs_here, length, q_heads, head_depth)
    key_rows_gradient = jnp.einsum(
        "skgqp,sqkgd->spkd", grad_scores, grouped_heads, preferred_element_type=jnp.float32
    )
    return (query_rows_gradient, key_rows_gradient, value_rows_gradient)


def normalize(hidden, pre_gain, pre_local):
    narrow = hidden.astype(jnp.float32)
    squares = one_axis_at_a_time(jnp.sum(narrow * narrow, axis=1), TENSOR)
    pre_scale = lax.rsqrt(squares[:, None] / pre_gain.shape[0] + NORM_EPS)
    normed = collect((narrow * pre_scale * pre_local).astype(jnp.bfloat16), TENSOR, 1)
    return (normed, pre_scale)


def attention_layer(hidden, normed, weights, adapters, lengths, post_local):
    w_query, w_key, value_projection, w_out, a_query, a_value = weights
    tok_rows, full_width = normed.shape
    seqs_here = lengths.shape[0]
    length = tok_rows // seqs_here
    query_rows = jnp.dot(normed, w_query, preferred_element_type=jnp.float32)
    keys_before_rotation = jnp.dot(normed, w_key, preferred_element_type=jnp.float32)
    value_rows = jnp.dot(normed, value_projection, preferred_element_type=jnp.float32)
    low_rank_update = None
    if adapters is not None:
        query_second_factor, value_second_factor = adapters
        rank_size = query_second_factor.shape[0]
        low_rank_update = jnp.dot(
            normed, jnp.concatenate([a_query, a_value], axis=1), preferred_element_type=jnp.float32
        ).astype(jnp.bfloat16)
        query_rows = query_rows + ADAPTER_SCALE * jnp.dot(
            low_rank_update[:, :rank_size], query_second_factor, preferred_element_type=jnp.float32
        )
        value_rows = value_rows + ADAPTER_SCALE * jnp.dot(
            low_rank_update[:, rank_size:], value_second_factor, preferred_element_type=jnp.float32
        )
    q_heads = query_rows.shape[1] // HEAD_SIZE
    kv_heads = keys_before_rotation.shape[1] // HEAD_SIZE
    query_rows = apply_rotation(
        query_rows.reshape(seqs_here, length, q_heads, HEAD_SIZE), 1.0
    ).astype(jnp.bfloat16)
    rotated_keys = apply_rotation(
        keys_before_rotation.reshape(seqs_here, length, kv_heads, HEAD_SIZE), 1.0
    ).astype(jnp.bfloat16)
    value_rows = value_rows.reshape(seqs_here, length, kv_heads, HEAD_SIZE).astype(jnp.bfloat16)
    mixed_out, probs_low, probabilities, capped = attend(
        query_rows, rotated_keys, value_rows, lengths
    )
    head_terms = lax.dot_general(
        mixed_out.reshape(tok_rows, q_heads * HEAD_SIZE),
        w_out,
        (((1,), (1,)), ((), ())),
        preferred_element_type=jnp.float32,
    )
    summed = summed_on_arrival(head_terms.astype(jnp.bfloat16), TENSOR, 1)
    squares = one_axis_at_a_time(jnp.sum(summed * summed, axis=1), TENSOR)
    post_scale = lax.rsqrt(squares[:, None] / full_width + NORM_EPS)
    result = hidden.astype(jnp.float32) + summed * post_scale * post_local
    saved = (
        low_rank_update,
        query_rows,
        rotated_keys,
        value_rows,
        probs_low,
        probabilities,
        capped,
        summed,
        post_scale,
    )
    return (result, saved)


def body(
    ref_hidden,
    pol_hidden,
    readout,
    lengths,
    pairing,
    pre_gain,
    post_gain,
    w_query,
    w_key,
    value_projection,
    w_out,
    a_query,
    a_value,
    query_second_factor,
    value_second_factor,
):
    tok_rows, part_width = pol_hidden.shape
    seqs_here = lengths.shape[0]
    length = tok_rows // seqs_here
    tensor_rank = lax.axis_index(TENSOR)
    data_rank = lax.axis_index(DP)
    all_seqs = seqs_here * lax.axis_size(DP)
    full_width = part_width * lax.axis_size(TENSOR)
    pre_local = lax.dynamic_slice_in_dim(pre_gain, tensor_rank * part_width, part_width)
    post_local = lax.dynamic_slice_in_dim(post_gain, tensor_rank * part_width, part_width)
    weights = sent_together((w_query, w_key, value_projection, w_out, a_query, a_value), DP, 0, 1)
    w_query_all, w_key_all, w_value_all, w_out_all, a_query_all, a_value_all = weights
    ref_normed, ref_scale = normalize(ref_hidden, pre_gain, pre_local)
    ref_result, ref_saved = attention_layer(
        ref_hidden, ref_normed, weights, None, lengths, post_local
    )
    pol_normed, pol_scale = normalize(pol_hidden, pre_gain, pre_local)
    pol_result, pol_saved = attention_layer(
        pol_hidden,
        pol_normed,
        weights,
        (query_second_factor, value_second_factor),
        lengths,
        post_local,
    )
    readout_wide = readout.astype(jnp.float32)
    living = (jnp.arange(length)[None, :] < lengths[:, None]).astype(jnp.float32)

    def sequence_score(result):
        return jnp.sum(
            jnp.sum(result * readout_wide, axis=1).reshape(seqs_here, length) * living, axis=1
        )

    placed = jnp.zeros((2, all_seqs), jnp.float32)
    offset = data_rank * seqs_here
    placed = lax.dynamic_update_slice(
        placed,
        jnp.stack([sequence_score(ref_result), sequence_score(pol_result)]),
        (jnp.int32(0), offset),
    )
    scores = one_axis_at_a_time(placed, DP_TENSOR)
    ratios = scores[1] - scores[0]
    chooser = (pairing[:, None] == jnp.arange(all_seqs)[None, :]).astype(jnp.float32)
    picked = jnp.dot(chooser, ratios, precision=lax.Precision.HIGHEST).reshape(-1, 2)
    margins = DPO_BETA * (picked[:, 0] - picked[:, 1])
    dpo_loss = jnp.sum(jax.nn.softplus(-margins))
    pair_pull = DPO_BETA * LOSS_SCALE * jax.nn.sigmoid(-margins)
    signed = jnp.stack([-pair_pull, pair_pull], axis=1).reshape(-1)
    coefficients = jnp.dot(signed, chooser, precision=lax.Precision.HIGHEST)
    local_coef = lax.dynamic_slice_in_dim(coefficients, offset, seqs_here)
    grad_result = (local_coef[:, None] * living).reshape(tok_rows, 1) * readout_wide
    (
        low_rank_update,
        query_rows,
        rotated_keys,
        value_rows,
        probs_low,
        probabilities,
        capped,
        summed,
        post_scale,
    ) = pol_saved
    post_dot = one_axis_at_a_time(jnp.sum(summed * post_local * grad_result, axis=1), TENSOR)
    grad_summed = (
        post_scale * post_local * grad_result
        - summed * post_scale**3 * post_dot[:, None] / full_width
    )
    grad_wide = collect(grad_summed.astype(jnp.bfloat16), TENSOR, 1)
    grad_mixed = jnp.dot(grad_wide, w_out_all, preferred_element_type=jnp.float32).astype(
        jnp.bfloat16
    )
    q_heads = query_rows.shape[2]
    grad_q_rot, rotated_key_gradient, value_head_gradient = attend_back(
        grad_mixed.reshape(seqs_here, length, q_heads, HEAD_SIZE),
        query_rows,
        rotated_keys,
        value_rows,
        probs_low,
        probabilities,
        capped,
    )
    query_rows_gradient = (
        apply_rotation(grad_q_rot, -1.0).reshape(tok_rows, -1).astype(jnp.bfloat16)
    )
    key_rows_gradient = (
        apply_rotation(rotated_key_gradient, -1.0).reshape(tok_rows, -1).astype(jnp.bfloat16)
    )
    value_rows_gradient = value_head_gradient.reshape(tok_rows, -1).astype(jnp.bfloat16)
    rank_size = query_second_factor.shape[0]
    rows_contraction = (((0,), (0,)), ((), ()))
    contract_cols = (((1,), (1,)), ((), ()))
    query_adapter_term = ADAPTER_SCALE * lax.dot_general(
        low_rank_update[:, :rank_size],
        query_rows_gradient,
        rows_contraction,
        preferred_element_type=jnp.float32,
    )
    value_adapter_term = ADAPTER_SCALE * lax.dot_general(
        low_rank_update[:, rank_size:],
        value_rows_gradient,
        rows_contraction,
        preferred_element_type=jnp.float32,
    )
    query_factor_gradient, value_factor_gradient = (
        over_copies(query_adapter_term.astype(jnp.bfloat16), DP).astype(jnp.float32),
        over_copies(value_adapter_term.astype(jnp.bfloat16), DP).astype(jnp.float32),
    )
    adapter_grad = jnp.concatenate(
        [
            ADAPTER_SCALE
            * lax.dot_general(
                query_rows_gradient,
                query_second_factor,
                contract_cols,
                preferred_element_type=jnp.float32,
            ),
            ADAPTER_SCALE
            * lax.dot_general(
                value_rows_gradient,
                value_second_factor,
                contract_cols,
                preferred_element_type=jnp.float32,
            ),
        ],
        axis=1,
    ).astype(jnp.bfloat16)
    adapter_term = lax.dot_general(
        pol_normed, adapter_grad, rows_contraction, preferred_element_type=jnp.float32
    )
    adapter_part = summed_on_arrival(adapter_term.astype(jnp.bfloat16), DP, 0)
    grad_a = lax.psum(adapter_part.astype(jnp.bfloat16), TENSOR).astype(jnp.float32)
    a_both = jnp.concatenate([a_query_all, a_value_all], axis=1)
    input_terms = lax.dot_general(
        query_rows_gradient, w_query_all, contract_cols, preferred_element_type=jnp.float32
    )
    input_terms = input_terms + lax.dot_general(
        key_rows_gradient, w_key_all, contract_cols, preferred_element_type=jnp.float32
    )
    input_terms = input_terms + lax.dot_general(
        value_rows_gradient, w_value_all, contract_cols, preferred_element_type=jnp.float32
    )
    input_terms = input_terms + lax.dot_general(
        adapter_grad, a_both, contract_cols, preferred_element_type=jnp.float32
    )
    input_whole = lax.psum(input_terms.astype(jnp.bfloat16), TENSOR).astype(jnp.float32)
    grad_normed = lax.dynamic_slice_in_dim(input_whole, tensor_rank * part_width, part_width, 1)
    narrow = pol_hidden.astype(jnp.float32)
    pre_dot = one_axis_at_a_time(jnp.sum(narrow * pre_local * grad_normed, axis=1), TENSOR)
    grad_hidden = (
        grad_result
        + pol_scale * pre_local * grad_normed
        - narrow * pol_scale**3 * pre_dot[:, None] / full_width
    )
    return (
        pol_result.astype(jnp.bfloat16),
        ref_result.astype(jnp.bfloat16),
        dpo_loss,
        grad_hidden.astype(jnp.bfloat16),
        grad_a,
        query_factor_gradient,
        value_factor_gradient,
    )


def solution(mesh):
    torus = Mesh(mesh.devices.reshape(4, 2, 4, 4), ("dp_0", "dp_1", "tensor_0", "tensor_1"))
    placed = (
        P(DP, TENSOR),
        P(DP, TENSOR),
        P(DP, TENSOR),
        P(DP),
        P(),
        P(),
        P(),
        P(DP, TENSOR),
        P(DP, TENSOR),
        P(DP, TENSOR),
        P(DP, TENSOR),
        P(DP, None),
        P(DP, None),
        P(None, TENSOR),
        P(None, TENSOR),
    )
    return jax.shard_map(
        body,
        mesh=torus,
        in_specs=placed,
        out_specs=(
            P(DP, TENSOR),
            P(DP, TENSOR),
            P(),
            P(DP, TENSOR),
            P(DP, None),
            P(None, TENSOR),
            P(None, TENSOR),
        ),
        check_vma=False,
    )
```

profile of v0, /device:TPU:0, one launch (start us, length us, event | category | flops | bytes accessed | tf_op | source)
XLA Modules:
  0.0 563.8 jit_solution(11571863054451459790)
XLA Ops:
  9.4 3.2 concatenate.55
  13.6 10.6 %all-reduce.3 = (f32[288]{0:T(512)S(1)}, f32[288]{0:T(512)S(1)}) all-reduce(f32[288]{0:T(512)S(1)} %get-tuple-element.60, f32[288]{0:T(512)S(1)} %get-tuple-element.59), channel_id=1, replica_groups=mesh['dp_0'=4,'dp_1'=2,'tensor_0'=4,'tensor_1'=4] {'tensor_0'}, use_global_device_ids=true, to_apply=%region_1.0 | all-reduce | flops 576 | bytes 4608 | tf_op jit(solution)/shard_map/psum | solution.py:23
  24.2 11.7 %all-reduce.1 = (f32[288]{0:T(512)S(1)}, f32[288]{0:T(512)S(1)}) all-reduce(f32[288]{0:T(512)S(1)} %get-tuple-element.17, f32[288]{0:T(512)S(1)} %get-tuple-element.18), channel_id=1, replica_groups=mesh['dp_0'=4,'dp_1'=2,'tensor_0'=4,'tensor_1'=4] {'tensor_1'}, use_global_device_ids=true, to_apply=%region_2.0 | all-reduce | flops 576 | bytes 4608 | tf_op jit(solution)/shard_map/psum | solution.py:23
  37.0 43.5 %all_to_all.40 = bf16[16,288,288]{2,1,0:T(8,128)(2,1)} all-to-all(bf16[16,288,288]{2,1,0:T(8,128)(2,1)S(1)} %broadcast_in_dim.31), channel_id=1, replica_groups=mesh['dp_0'=4,'dp_1'=2,'tensor_0'=4,'tensor_1'=4] {'tensor_0','tensor_1'}, dimensions={0} | all-to-all | bytes 5308416 | tf_op jit(solution)/shard_map/all_to_all | solution.py:28
  80.6 2.1 broadcast_in_dim.24
  82.7 4.6 all-to-all-start
  89.0 5.1 copy.96
  94.2 6.7 %dot_general.122 = bf16[3,96,4608]{2,1,0:T(8,128)(2,1)} reshape(bf16[288,16,288]{2,1,0:T(8,128)(2,1)} %copy.96) | data formatting | bytes 5308416 | tf_op jit(solution)/shard_map/dot_general | solution.py:161
  100.8 6.6 %reshape.391 = bf16[3,96,4608,1]{2,1,0,3:T(8,128)(2,1)} reshape(bf16[288,16,288]{2,1,0:T(8,128)(2,1)} %copy.96) | data formatting | bytes 5308416 | tf_op jit(solution)/shard_map/dot_general | solution.py:161
  107.5 21.0 %all-to-all-done = bf16[16,288,288]{2,1,0:T(8,128)(2,1)} async-done(((bf16[16,288,288]{2,1,0:T(8,128)(2,1)}), bf16[16,288,288]{2,1,0:T(8,128)(2,1)}, u32[]{:S(2)}, u32[]{:S(2)}) %all-to-all-start) | async-done | bytes 2654240 | tf_op jit(solution)/shard_map/all_to_all | solution.py:28
  128.5 5.1 copy.87
  133.5 5.6 reshape.369
  139.1 7.2 %dot_general.114 = bf16[3,96,4608]{2,1,0:T(8,128)(2,1)} reshape(bf16[288,16,288]{2,1,0:T(8,128)(2,1)} %copy.87) | data formatting | bytes 5308416 | tf_op jit(solution)/shard_map/dot_general | solution.py:160
  146.3 3.2 slice_bitcast_fusion
  149.5 4.8 copy.119
  154.3 2.1 convolution_convert_fusion.5
  157.3 2.5 fusion.9
  162.2 3.5 fusion.1
  165.7 2.3 fusion.32
  168.0 2.1 fusion.29
  173.0 2.2 fusion.35
  175.9 2.5 convolution_convert_fusion.1
  178.4 5.9 %reshape.372 = bf16[288,16,288]{2,1,0:T(8,128)(2,1)} reshape(bf16[288,4608]{1,0:T(8,128)(2,1)S(1)} %convolution_convert_fusion.1) | data formatting | bytes 5308416 | tf_op jit(solution)/shard_map/reshape | solution.py:46
  184.3 4.5 copy.158
  188.9 9.0 %all-to-all-start.1 = ((bf16[16,288,288]{2,1,0:T(8,128)(2,1)}), bf16[16,288,288]{2,1,0:T(8,128)(2,1)}, u32[]{:S(2)}, u32[]{:S(2)}) async-start(bf16[16,288,288]{2,1,0:T(8,128)(2,1)} %bitcast.230), calls=%async_computation.1 | async-start | bytes 7077888 | tf_op jit(solution)/shard_map/all_to_all | solution.py:52
  197.9 2.6 fusion.136
  200.5 2.4 fusion.28
  203.0 2.6 convolution_convert_fusion
  205.6 5.9 %reshape.374 = bf16[288,16,288]{2,1,0:T(8,128)(2,1)} reshape(bf16[288,4608]{1,0:T(8,128)(2,1)S(1)} %convolution_convert_fusion) | data formatting | bytes 5308416 | tf_op jit(solution)/shard_map/reshape | solution.py:46
  211.4 4.6 copy.157
  216.0 25.3 %all-to-all-done.1 = bf16[16,288,288]{2,1,0:T(8,128)(2,1)} async-done(((bf16[16,288,288]{2,1,0:T(8,128)(2,1)}), bf16[16,288,288]{2,1,0:T(8,128)(2,1)}, u32[]{:S(2)}, u32[]{:S(2)}) %all-to-all-start.1) | async-done | bytes 2654240 | tf_op jit(solution)/shard_map/all_to_all | solution.py:52
  241.3 6.2 %all-to-all-start.3 = ((bf16[16,288,288]{2,1,0:T(8,128)(2,1)}), bf16[16,288,288]{2,1,0:T(8,128)(2,1)}, u32[]{:S(2)}, u32[]{:S(2)}) async-start(bf16[16,288,288]{2,1,0:T(8,128)(2,1)} %bitcast.229), calls=%async_computation.3 | async-start | bytes 7077888 | tf_op jit(solution)/shard_map/all_to_all | solution.py:52
  248.5 2.6 convert_reduce_fusion.1
  251.3 39.3 %all-to-all-done.3 = bf16[16,288,288]{2,1,0:T(8,128)(2,1)} async-done(((bf16[16,288,288]{2,1,0:T(8,128)(2,1)}), bf16[16,288,288]{2,1,0:T(8,128)(2,1)}, u32[]{:S(2)}, u32[]{:S(2)}) %all-to-all-start.3) | async-done | bytes 2654240 | tf_op jit(solution)/shard_map/all_to_all | solution.py:52
  290.6 2.6 convert_reduce_fusion
  293.4 9.2 %all-reduce.2 = (f32[288]{0:T(512)S(1)}, f32[288]{0:T(512)S(1)}) all-reduce(f32[288]{0:T(512)S(1)} %multiply_reduce_fusion.1, f32[288]{0:T(512)S(1)} %multiply_reduce_fusion), channel_id=1, replica_groups=mesh['dp_0'=4,'dp_1'=2,'tensor_0'=4,'tensor_1'=4] {'tensor_0'}, use_global_device_ids=true, to_apply=%region_6.7 | all-reduce | flops 576 | bytes 4608 | tf_op jit(solution)/shard_map/psum | solution.py:23
  302.6 9.1 %all-reduce = (f32[288]{0:T(512)S(1)}, f32[288]{0:T(512)S(1)}) all-reduce(f32[288]{0:T(512)S(1)} %get-tuple-element.15, f32[288]{0:T(512)S(1)} %get-tuple-element.16), channel_id=1, replica_groups=mesh['dp_0'=4,'dp_1'=2,'tensor_0'=4,'tensor_1'=4] {'tensor_1'}, use_global_device_ids=true, to_apply=%region_7.8 | all-reduce | flops 576 | bytes 4608 | tf_op jit(solution)/shard_map/psum | solution.py:23
  313.3 11.4 %psum.134 = f32[2,24]{1,0:T(2,128)S(1)} all-reduce(f32[2,24]{1,0:T(2,128)S(1)} %dynamic_update_slice.3), channel_id=1, replica_groups=mesh['dp_0'=4,'dp_1'=2,'tensor_0'=4,'tensor_1'=4] {'dp_0'}, use_global_device_ids=true, to_apply=%region_20.21 | all-reduce | flops 48 | bytes 384 | tf_op jit(solution)/shard_map/psum | solution.py:23
  324.8 2.5 psum.135
  327.2 8.9 %psum.136 = f32[2,24]{1,0:T(2,128)S(1)} all-reduce(f32[2,24]{1,0:T(2,128)S(1)} %psum.135), channel_id=1, replica_groups=mesh['dp_0'=4,'dp_1'=2,'tensor_0'=4,'tensor_1'=4] {'tensor_0'}, use_global_device_ids=true, to_apply=%region_22.23 | all-reduce | flops 48 | bytes 384 | tf_op jit(solution)/shard_map/psum | solution.py:23
  336.2 7.7 %psum.137 = f32[2,24]{1,0:T(2,128)S(1)} all-reduce(f32[2,24]{1,0:T(2,128)S(1)} %psum.136), channel_id=1, replica_groups=mesh['dp_0'=4,'dp_1'=2,'tensor_0'=4,'tensor_1'=4] {'tensor_1'}, use_global_device_ids=true, to_apply=%region_23.24 | all-reduce | flops 48 | bytes 384 | tf_op jit(solution)/shard_map/psum | solution.py:23
  345.0 8.5 %psum.138 = f32[288]{0:T(512)S(1)} all-reduce(f32[288]{0:T(512)S(1)} %fusion.63), channel_id=1, replica_groups=mesh['dp_0'=4,'dp_1'=2,'tensor_0'=4,'tensor_1'=4] {'tensor_0'}, use_global_device_ids=true, to_apply=%region_26.27 | all-reduce | flops 288 | bytes 2304 | tf_op jit(solution)/shard_map/psum | solution.py:23
  353.6 9.8 %psum.139 = f32[288]{0:T(512)S(1)} all-reduce(f32[288]{0:T(512)S(1)} %psum.138), channel_id=1, replica_groups=mesh['dp_0'=4,'dp_1'=2,'tensor_0'=4,'tensor_1'=4] {'tensor_1'}, use_global_device_ids=true, to_apply=%region_27.28 | all-reduce | flops 288 | bytes 2304 | tf_op jit(solution)/shard_map/psum | solution.py:23
  363.9 39.1 %all_to_all.41 = bf16[16,288,288]{2,1,0:T(8,128)(2,1)S(1)} all-to-all(bf16[16,288,288]{2,1,0:T(8,128)(2,1)S(1)} %broadcast_in_dim.33), channel_id=1, replica_groups=mesh['dp_0'=4,'dp_1'=2,'tensor_0'=4,'tensor_1'=4] {'tensor_0','tensor_1'}, dimensions={0} | all-to-all | bytes 5308416 | tf_op jit(solution)/shard_map/all_to_all | solution.py:28
  403.0 3.1 copy.103
  406.1 6.7 %reshape.378 = bf16[288,4608]{1,0:T(8,128)(2,1)} reshape(bf16[288,16,288]{2,1,0:T(8,128)(2,1)} %copy.103) | data formatting | bytes 5308416 | tf_op jit(solution)/shard_map/reshape | solution.py:36
  412.7 3.4 fusion.23
  418.6 2.2 convolution_convert_fusion.2
  420.8 3.6 all-to-all-start.5
  424.5 2.6 fusion.7
  427.1 2.2 convolution_add_fusion.2
  429.3 2.1 convolution_add_fusion.1
  431.4 3.8 fusion
  435.2 6.4 %all-to-all-done.5 = bf16[8,576,128]{2,1,0:T(8,128)(2,1)S(1)} async-done(((bf16[8,576,128]{2,1,0:T(8,128)(2,1)}), bf16[8,576,128]{2,1,0:T(8,128)(2,1)S(1)}, u32[]{:S(2)}, u32[]{:S(2)}) %all-to-all-start.5) | async-done | bytes 1179680 | tf_op jit(solution)/shard_map/all_to_all | solution.py:52
  443.5 3.4 all-to-all-start.7
  447.0 5.8 %all-to-all-done.7 = bf16[8,64,128]{2,1,0:T(8,128)(2,1)S(1)} async-done(((bf16[8,64,128]{2,1,0:T(8,128)(2,1)}), bf16[8,64,128]{2,1,0:T(8,128)(2,1)S(1)}, u32[]{:S(2)}, u32[]{:S(2)}) %all-to-all-start.7) | async-done | bytes 131104 | tf_op jit(solution)/shard_map/all_to_all | solution.py:28
  453.6 3.4 all-to-all-start.6
  458.3 6.2 %all-to-all-done.6 = bf16[8,64,256]{2,1,0:T(8,128)(2,1)S(1)} async-done(((bf16[8,64,256]{2,1,0:T(8,128)(2,1)}), bf16[8,64,256]{2,1,0:T(8,128)(2,1)S(1)}, u32[]{:S(2)}, u32[]{:S(2)}) %all-to-all-start.6) | async-done | bytes 262176 | tf_op jit(solution)/shard_map/all_to_all | solution.py:28
  465.1 68.0 %all-reduce.7.cloned.1.call-done = (bf16[288,4608]{1,0:T(8,128)(2,1)}, bf16[576,128]{1,0:T(8,128)(2,1)}) async-done(((bf16[288,4608]{1,0:T(8,128)(2,1)}, bf16[576,128]{1,0:T(8,128)(2,1)}), (bf16[288,4608]{1,0:T(8,128)(2,1)}, bf16[576,128]{1,0:T(8,128)(2,1)})) %all-reduce.7.cloned.1.call-update) | async-done | bytes 2801680 | tf_op jit(solution)/shard_map/psum | solution.py:371
  533.1 1.2 fusion.60
  534.3 10.0 %psum.141 = f32[288]{0:T(512)S(1)} all-reduce(f32[288]{0:T(512)S(1)} %fusion.60), channel_id=1, replica_groups=mesh['dp_0'=4,'dp_1'=2,'tensor_0'=4,'tensor_1'=4] {'tensor_0'}, use_global_device_ids=true, to_apply=%region_31.32 | all-reduce | flops 288 | bytes 2304 | tf_op jit(solution)/shard_map/psum | solution.py:23
  544.3 8.8 %psum.142 = f32[288]{0:T(512)S(1)} all-reduce(f32[288]{0:T(512)S(1)} %psum.141), channel_id=1, replica_groups=mesh['dp_0'=4,'dp_1'=2,'tensor_0'=4,'tensor_1'=4] {'tensor_1'}, use_global_device_ids=true, to_apply=%region_32.33 | all-reduce | flops 288 | bytes 2304 | tf_op jit(solution)/shard_map/psum | solution.py:23
  553.0 1.6 convert_element_type.190
  554.7 2.0 fusion.65
  (147 shorter events, 24.4 us)
Async XLA Ops:
  7.2 152.7 %copy-start = (bf16[64,256]{1,0:T(8,128)(2,1)S(1)}, bf16[64,256]{1,0:T(8,128)(2,1)}, u32[]{:S(2)}) copy-start(bf16[64,256]{1,0:T(8,128)(2,1)} %param.28) | copy-start | bytes 98308
  7.2 6.2 %copy-start.3 = (bf16[288,288]{1,0:T(8,128)(2,1)S(1)}, bf16[288,288]{1,0:T(8,128)(2,1)}, u32[]{:S(2)}) copy-start(bf16[288,288]{1,0:T(8,128)(2,1)} %param.16) | copy-start | bytes 497668
  7.2 6.2 %copy-start.8 = (bf16[288,288]{1,0:T(8,128)(2,1)S(1)}, bf16[288,288]{1,0:T(8,128)(2,1)}, u32[]{:S(2)}) copy-start(bf16[288,288]{1,0:T(8,128)(2,1)} %param.15) | copy-start | bytes 497668
  7.2 139.1 %all-gather.2.cloned.1.call-start = ((), (), s32[]{:S(2)}) async-start(), calls=%async_computation.8 | async-start | bytes 9289728 | tf_op jit(solution)/shard_map/all_gather | solution.py:62
  82.7 4.7 copy-start.31
  82.7 45.8 %all-to-all-start = ((bf16[16,288,288]{2,1,0:T(8,128)(2,1)}), bf16[16,288,288]{2,1,0:T(8,128)(2,1)}, u32[]{:S(2)}, u32[]{:S(2)}) async-start(bf16[16,288,288]{2,1,0:T(8,128)(2,1)} %broadcast_in_dim.24), calls=%async_computation | async-start | bytes 7077888 | tf_op jit(solution)/shard_map/all_to_all | solution.py:28
  139.1 33.9 %copy-start.1 = (bf16[288,4608]{1,0:T(8,128)(2,1)}, bf16[288,4608]{1,0:T(8,128)(2,1)S(1)}, u32[]{:S(2)}) copy-start(bf16[288,4608]{1,0:T(8,128)(2,1)S(1)} %reshape.369) | copy-start | bytes 7962628
  154.3 2.1 copy-start.26
  162.2 3.5 copy-start.5
  165.7 2.3 copy-start.7
  168.0 2.2 copy-start.14
  170.2 2.5 copy-start.23
  170.2 2.8 copy-start.25
  171.0 0.9 copy-start.17
  171.0 0.9 copy-start.19
  171.9 0.7 copy-start.9
  171.9 0.7 copy-start.11
  173.0 2.3 copy-start.15
  173.0 2.3 copy-start.29
  175.3 0.6 copy-start.34
  188.9 9.0 %copy-start.21 = (bf16[3,96,2,64]{3,1,2,0:T(8,128)(2,1)S(1)}, bf16[3,96,2,64]{3,1,2,0:T(8,128)(2,1)}, u32[]{:S(2)}) copy-start(bf16[3,96,2,64]{3,1,2,0:T(8,128)(2,1)} %get-tuple-element.30) | copy-start | bytes 221188
  188.9 9.0 %copy-start.22 = (bf16[3,96,2,64]{3,1,2,0:T(8,128)(2,1)S(1)}, bf16[3,96,2,64]{3,1,2,0:T(8,128)(2,1)}, u32[]{:S(2)}) copy-start(bf16[3,96,2,64]{3,1,2,0:T(8,128)(2,1)} %get-tuple-element.31) | copy-start | bytes 221188
  188.9 11.6 %copy-start.6 = (bf16[3,96,4608]{2,1,0:T(8,128)(2,1)S(1)}, bf16[3,96,4608]{2,1,0:T(8,128)(2,1)}, u32[]{:S(2)}) copy-start(bf16[3,96,4608]{2,1,0:T(8,128)(2,1)} %dot_general.122) | copy-start | bytes 7962628
  188.9 52.4 %all-to-all-start.1 = ((bf16[16,288,288]{2,1,0:T(8,128)(2,1)}), bf16[16,288,288]{2,1,0:T(8,128)(2,1)}, u32[]{:S(2)}, u32[]{:S(2)}) async-start(bf16[16,288,288]{2,1,0:T(8,128)(2,1)} %bitcast.230), calls=%async_computation.1 | async-start | bytes 7077888 | tf_op jit(solution)/shard_map/all_to_all | solution.py:52
  241.3 7.0 %copy-start.33 = (s32[24]{0:T(128)S(1)}, s32[24]{0:T(128)}, u32[]{:S(2)}) copy-start(s32[24]{0:T(128)} %param.19) | copy-start | bytes 292
  241.3 49.3 %all-to-all-start.3 = ((bf16[16,288,288]{2,1,0:T(8,128)(2,1)}), bf16[16,288,288]{2,1,0:T(8,128)(2,1)}, u32[]{:S(2)}, u32[]{:S(2)}) async-start(bf16[16,288,288]{2,1,0:T(8,128)(2,1)} %bitcast.229), calls=%async_computation.3 | async-start | bytes 7077888 | tf_op jit(solution)/shard_map/all_to_all | solution.py:52
  251.1 60.5 %copy-start.4 = (bf16[288,288]{1,0:T(8,128)(2,1)S(1)}, bf16[288,288]{1,0:T(8,128)(2,1)}, u32[]{:S(2)}) copy-start(bf16[288,288]{1,0:T(8,128)(2,1)} %param.17) | copy-start | bytes 497668
  251.3 61.6 %copy-start.32 = (s32[3]{0:T(128)S(1)}, s32[3]{0:T(128)}, u32[]{:S(2)}) copy-start(s32[3]{0:T(128)} %param.18) | copy-start | bytes 40
  412.7 3.5 copy-start.16
  412.7 3.5 copy-start.24
  412.7 3.5 copy-start.30
  412.7 3.8 copy-start.35
  416.1 0.9 copy-start.10
  416.1 1.0 copy-start.12
  416.1 1.2 copy-start.18
  416.1 1.2 copy-start.20
  416.2 1.4 copy-start.27
  416.2 1.6 copy-start.13
  416.8 1.8 copy-start.2
  420.8 20.8 %all-to-all-start.5 = ((bf16[8,576,128]{2,1,0:T(8,128)(2,1)}), bf16[8,576,128]{2,1,0:T(8,128)(2,1)S(1)}, u32[]{:S(2)}, u32[]{:S(2)}) async-start(bf16[8,576,128]{2,1,0:T(8,128)(2,1)} %bitcast.71), calls=%async_computation.5 | async-start | bytes 2359296 | tf_op jit(solution)/shard_map/all_to_all | solution.py:52
  424.4 108.7 %all-reduce.7.cloned.1.call-start = ((), (), s32[]{:S(2)}) async-start(), calls=%async_computation.9 | async-start | bytes 5603328 | tf_op jit(solution)/shard_map/psum | solution.py:371
  442.5 112.2 %copy-start.28 = (f32[288]{0:T(512)S(1)}, f32[288]{0:T(512)}, u32[]{:S(2)}) copy-start(f32[288]{0:T(512)} %get-tuple-element.44) | copy-start | bytes 3460
  443.5 9.4 %all-to-all-start.7 = ((bf16[8,64,128]{2,1,0:T(8,128)(2,1)}), bf16[8,64,128]{2,1,0:T(8,128)(2,1)S(1)}, u32[]{:S(2)}, u32[]{:S(2)}) async-start(bf16[8,64,128]{2,1,0:T(8,128)(2,1)} %broadcast_in_dim.35), calls=%async_computation.7 | async-start | bytes 262144 | tf_op jit(solution)/shard_map/all_to_all | solution.py:28
  453.6 10.9 %all-to-all-start.6 = ((bf16[8,64,256]{2,1,0:T(8,128)(2,1)}), bf16[8,64,256]{2,1,0:T(8,128)(2,1)S(1)}, u32[]{:S(2)}, u32[]{:S(2)}) async-start(bf16[8,64,256]{2,1,0:T(8,128)(2,1)} %broadcast_in_dim.34), calls=%async_computation.6 | async-start | bytes 524288 | tf_op jit(solution)/shard_map/all_to_all | solution.py:28
Sparse Core Ops, SparseCore 0:
  12.7 51.5 all-gather.1
  442.6 90.4 all-reduce.6
where the time goes:
time: 573 us; the launch traced here: 564 us
  blocking collectives  191 us (33%)
  waiting for transfers between devices  172 us (30%)
  local copies, waits for them, and re-layouts  89.7 us (16%)
  matrix products  45.7 us (8%)
  starting transfers between devices  30.3 us (5%)
  other arithmetic  20.1 us (4%)
  between operations  15 us (3%)
    psum x12, blocking collectives, one_axis_at_a_time(): return functools.reduce(lax.psum, axes, shard)  108 us
    all_to_all x2, blocking collectives, copy_for_each(): lax.all_to_all(jnp.broadcast_to(shard[None], (count, *shard.shape)), axis...  82.7 us
    all_to_all x3, waiting for transfers between devices, summed_on_arrival(): lax.all_to_all(tiles, axis, split_axis=0, concat_axis=0, tiled=True)  71.1 us
    psum x1, waiting for transfers between devices, body(): lax.psum(input_terms.astype(jnp.bfloat16), TENSOR).astype(jnp.float32)  68 us
    all_to_all x3, waiting for transfers between devices, copy_for_each(): lax.all_to_all(jnp.broadcast_to(shard[None], (count, *shard.shape)), axis...  33 us
    reshape x4, local copies, waits for them, and re-layouts, split_up(): shard.reshape(*shape[:dim], count, shape[dim] // count, *shape[dim + 1:])  20.9 us
    all_to_all x3, starting transfers between devices, summed_on_arrival(): lax.all_to_all(tiles, axis, split_axis=0, concat_axis=0, tiled=True)  18.8 us
    dot_general x2, local copies, waits for them, and re-layouts, attention_layer(): jnp.dot(normed, value_projection, preferred_element_type=jnp.float32)  13.3 us
  transfers between devices with their start and end apart: 8, of which 7 were waited for; matrix products, arithmetic and copies ran while one was open for 14% of the time, Pallas kernels for 0%

commit v1 on v0

--- a/solution.py
+++ b/solution.py
@@ -368,7 +368,9 @@
     input_terms = input_terms + lax.dot_general(
         adapter_grad, a_both, contract_cols, preferred_element_type=jnp.float32
     )
-    input_whole = lax.psum(input_terms.astype(jnp.bfloat16), TENSOR).astype(jnp.float32)
+    input_whole = jnp.sum(lax.all_gather(input_terms.astype(jnp.bfloat16), TENSOR), axis=0).astype(
+        jnp.float32
+    )
     grad_normed = lax.dynamic_slice_in_dim(input_whole, tensor_rank * part_width, part_width, 1)
     narrow = pol_hidden.astype(jnp.float32)
     pre_dot = one_axis_at_a_time(jnp.sum(narrow * pre_local * grad_normed, axis=1), TENSOR)

time: 573 us -> 820 us (1.43)
  waiting for transfers between devices: 172 us -> 400 us
  other arithmetic: 20.1 us -> 33 us
    all_gather x0 -> x1, waiting for transfers between devices: none -> 242 us  [body(): lax.all_gather(input_terms.astype(jnp.bfloat16), TENSOR)]
    psum x1, waiting for transfers between devices: 68 us -> 52.8 us  [body(): lax.psum(adapter_part.astype(jnp.bfloat16), TENSOR).astype(jnp.float32)]
    reduce_sum x0 -> x1, other arithmetic: none -> 14.3 us  [body(): jnp.sum(lax.all_gather(input_terms.astype(jnp.bfloat16), TENSOR), axis=0)]
  transfers between devices with their start and end apart: 8 -> 9, of which waited for: 7 -> 8; matrix products, arithmetic and copies ran while one was open for 14% -> 10% of each run, Pallas kernels for 0% -> 0%
where the time goes in v1:
time: 820 us; the launch traced here: 811 us
  waiting for transfers between devices  400 us (49%)
  blocking collectives  191 us (23%)
  local copies, waits for them, and re-layouts  89.8 us (11%)
  matrix products  51.4 us (6%)
  other arithmetic  33 us (4%)
  starting transfers between devices  30.4 us (4%)
  between operations  14.7 us (2%)
    all_gather x1, waiting for transfers between devices, body(): lax.all_gather(input_terms.astype(jnp.bfloat16), TENSOR)  242 us
    psum x12, blocking collectives, one_axis_at_a_time(): return functools.reduce(lax.psum, axes, shard)  108 us
    all_to_all x2, blocking collectives, copy_for_each(): lax.all_to_all(jnp.broadcast_to(shard[None], (count, *shard.shape)), axis...  82.6 us
    all_to_all x3, waiting for transfers between devices, summed_on_arrival(): lax.all_to_all(tiles, axis, split_axis=0, concat_axis=0, tiled=True)  72.4 us
    psum x1, waiting for transfers between devices, body(): lax.psum(adapter_part.astype(jnp.bfloat16), TENSOR).astype(jnp.float32)  52.8 us
    all_to_all x3, waiting for transfers between devices, copy_for_each(): lax.all_to_all(jnp.broadcast_to(shard[None], (count, *shard.shape)), axis...  33.1 us
    reshape x4, local copies, waits for them, and re-layouts, split_up(): shard.reshape(*shape[:dim], count, shape[dim] // count, *shape[dim + 1:])  21 us
    all_to_all x3, starting transfers between devices, summed_on_arrival(): lax.all_to_all(tiles, axis, split_axis=0, concat_axis=0, tiled=True)  18.8 us
  transfers between devices with their start and end apart: 9, of which 8 were waited for; matrix products, arithmetic and copies ran while one was open for 10% of the time, Pallas kernels for 0%

profile of v1, /device:TPU:0, one launch (start us, length us, event | category | flops | bytes accessed | tf_op | source)
XLA Modules:
  0.0 810.8 jit_solution(10329011098672244443)
XLA Ops:
  9.4 3.2 concatenate.55
  13.6 10.6 %all-reduce.3 = (f32[288]{0:T(512)S(1)}, f32[288]{0:T(512)S(1)}) all-reduce(f32[288]{0:T(512)S(1)} %get-tuple-element.58, f32[288]{0:T(512)S(1)} %get-tuple-element.57), channel_id=1, replica_groups=mesh['dp_0'=4,'dp_1'=2,'tensor_0'=4,'tensor_1'=4] {'tensor_0'}, use_global_device_ids=true, to_apply=%region_1.0 | all-reduce | flops 576 | bytes 4608 | tf_op jit(solution)/shard_map/psum | solution.py:23
  24.2 11.7 %all-reduce.1 = (f32[288]{0:T(512)S(1)}, f32[288]{0:T(512)S(1)}) all-reduce(f32[288]{0:T(512)S(1)} %get-tuple-element.17, f32[288]{0:T(512)S(1)} %get-tuple-element.18), channel_id=1, replica_groups=mesh['dp_0'=4,'dp_1'=2,'tensor_0'=4,'tensor_1'=4] {'tensor_1'}, use_global_device_ids=true, to_apply=%region_2.0 | all-reduce | flops 576 | bytes 4608 | tf_op jit(solution)/shard_map/psum | solution.py:23
  37.1 43.5 %all_to_all.40 = bf16[16,288,288]{2,1,0:T(8,128)(2,1)} all-to-all(bf16[16,288,288]{2,1,0:T(8,128)(2,1)S(1)} %broadcast_in_dim.31), channel_id=1, replica_groups=mesh['dp_0'=4,'dp_1'=2,'tensor_0'=4,'tensor_1'=4] {'tensor_0','tensor_1'}, dimensions={0} | all-to-all | bytes 5308416 | tf_op jit(solution)/shard_map/all_to_all | solution.py:28
  80.6 2.2 broadcast_in_dim.24
  82.7 4.7 all-to-all-start
  89.1 5.1 copy.96
  94.2 6.6 dot_general.122
  100.8 6.6 reshape.392
  107.5 21.1 %all-to-all-done = bf16[16,288,288]{2,1,0:T(8,128)(2,1)} async-done(((bf16[16,288,288]{2,1,0:T(8,128)(2,1)}), bf16[16,288,288]{2,1,0:T(8,128)(2,1)}, u32[]{:S(2)}, u32[]{:S(2)}) %all-to-all-start) | async-done | bytes 2654240 | tf_op jit(solution)/shard_map/all_to_all | solution.py:28
  128.6 5.1 copy.87
  133.7 5.6 reshape.369
  139.3 7.2 dot_general.114
  146.5 3.2 slice_bitcast_fusion
  149.7 4.7 copy.119
  154.4 2.1 convolution_convert_fusion.5
  157.5 2.5 fusion.9
  162.4 3.5 fusion.1
  165.9 2.3 fusion.32
  168.2 2.1 fusion.29
  173.2 2.2 fusion.35
  176.1 2.5 convolution_convert_fusion.1
  178.7 5.9 reshape.372
  184.5 4.6 copy.158
  189.2 9.0 %all-to-all-start.1 = ((bf16[16,288,288]{2,1,0:T(8,128)(2,1)}), bf16[16,288,288]{2,1,0:T(8,128)(2,1)}, u32[]{:S(2)}, u32[]{:S(2)}) async-start(bf16[16,288,288]{2,1,0:T(8,128)(2,1)} %bitcast.232), calls=%async_computation.1 | async-start | bytes 7077888 | tf_op jit(solution)/shard_map/all_to_all | solution.py:52
  198.2 2.6 fusion.136
  200.8 2.4 fusion.28
  203.3 2.6 convolution_convert_fusion
  205.9 5.9 reshape.374
  211.8 4.6 copy.157
  216.3 25.3 %all-to-all-done.1 = bf16[16,288,288]{2,1,0:T(8,128)(2,1)} async-done(((bf16[16,288,288]{2,1,0:T(8,128)(2,1)}), bf16[16,288,288]{2,1,0:T(8,128)(2,1)}, u32[]{:S(2)}, u32[]{:S(2)}) %all-to-all-start.1) | async-done | bytes 2654240 | tf_op jit(solution)/shard_map/all_to_all | solution.py:52
  241.6 6.2 all-to-all-start.3
  248.8 2.6 convert_reduce_fusion.1
  251.6 39.3 %all-to-all-done.3 = bf16[16,288,288]{2,1,0:T(8,128)(2,1)} async-done(((bf16[16,288,288]{2,1,0:T(8,128)(2,1)}), bf16[16,288,288]{2,1,0:T(8,128)(2,1)}, u32[]{:S(2)}, u32[]{:S(2)}) %all-to-all-start.3) | async-done | bytes 2654240 | tf_op jit(solution)/shard_map/all_to_all | solution.py:52
  290.9 2.6 convert_reduce_fusion
  293.7 9.2 %all-reduce.2 = (f32[288]{0:T(512)S(1)}, f32[288]{0:T(512)S(1)}) all-reduce(f32[288]{0:T(512)S(1)} %multiply_reduce_fusion.1, f32[288]{0:T(512)S(1)} %multiply_reduce_fusion), channel_id=1, replica_groups=mesh['dp_0'=4,'dp_1'=2,'tensor_0'=4,'tensor_1'=4] {'tensor_0'}, use_global_device_ids=true, to_apply=%region_6.7 | all-reduce | flops 576 | bytes 4608 | tf_op jit(solution)/shard_map/psum | solution.py:23
  302.8 9.1 %all-reduce = (f32[288]{0:T(512)S(1)}, f32[288]{0:T(512)S(1)}) all-reduce(f32[288]{0:T(512)S(1)} %get-tuple-element.15, f32[288]{0:T(512)S(1)} %get-tuple-element.16), channel_id=1, replica_groups=mesh['dp_0'=4,'dp_1'=2,'tensor_0'=4,'tensor_1'=4] {'tensor_1'}, use_global_device_ids=true, to_apply=%region_7.8 | all-reduce | flops 576 | bytes 4608 | tf_op jit(solution)/shard_map/psum | solution.py:23
  313.6 11.4 %psum.127 = f32[2,24]{1,0:T(2,128)S(1)} all-reduce(f32[2,24]{1,0:T(2,128)S(1)} %dynamic_update_slice.3), channel_id=1, replica_groups=mesh['dp_0'=4,'dp_1'=2,'tensor_0'=4,'tensor_1'=4] {'dp_0'}, use_global_device_ids=true, to_apply=%region_20.21 | all-reduce | flops 48 | bytes 384 | tf_op jit(solution)/shard_map/psum | solution.py:23
  325.0 2.5 psum.128
  327.5 8.7 %psum.129 = f32[2,24]{1,0:T(2,128)S(1)} all-reduce(f32[2,24]{1,0:T(2,128)S(1)} %psum.128), channel_id=1, replica_groups=mesh['dp_0'=4,'dp_1'=2,'tensor_0'=4,'tensor_1'=4] {'tensor_0'}, use_global_device_ids=true, to_apply=%region_22.23 | all-reduce | flops 48 | bytes 384 | tf_op jit(solution)/shard_map/psum | solution.py:23
  336.1 7.7 psum.130
  345.5 8.8 %psum.131 = f32[288]{0:T(512)S(1)} all-reduce(f32[288]{0:T(512)S(1)} %fusion.63), channel_id=1, replica_groups=mesh['dp_0'=4,'dp_1'=2,'tensor_0'=4,'tensor_1'=4] {'tensor_0'}, use_global_device_ids=true, to_apply=%region_26.27 | all-reduce | flops 288 | bytes 2304 | tf_op jit(solution)/shard_map/psum | solution.py:23
  354.3 9.8 %psum.132 = f32[288]{0:T(512)S(1)} all-reduce(f32[288]{0:T(512)S(1)} %psum.131), channel_id=1, replica_groups=mesh['dp_0'=4,'dp_1'=2,'tensor_0'=4,'tensor_1'=4] {'tensor_1'}, use_global_device_ids=true, to_apply=%region_27.28 | all-reduce | flops 288 | bytes 2304 | tf_op jit(solution)/shard_map/psum | solution.py:23
  364.6 39.1 %all_to_all.41 = bf16[16,288,288]{2,1,0:T(8,128)(2,1)S(1)} all-to-all(bf16[16,288,288]{2,1,0:T(8,128)(2,1)S(1)} %broadcast_in_dim.33), channel_id=1, replica_groups=mesh['dp_0'=4,'dp_1'=2,'tensor_0'=4,'tensor_1'=4] {'tensor_0','tensor_1'}, dimensions={0} | all-to-all | bytes 5308416 | tf_op jit(solution)/shard_map/all_to_all | solution.py:28
  403.8 3.2 copy.103
  406.9 5.6 reshape.378
  412.5 3.2 fusion.23
  421.1 2.2 convolution_convert_fusion.2
  423.3 3.6 all-to-all-start.5
  427.0 2.6 fusion.7
  429.6 2.1 convolution_add_fusion.2
  431.7 4.6 convolution_add_fusion.1
  436.3 7.8 all-to-all-done.5
  445.0 5.3 fusion
  451.3 3.4 all-to-all-start.7
  454.9 5.8 all-to-all-done.7
  461.4 3.4 all-to-all-start.6
  466.1 6.2 all-to-all-done.6
  472.9 52.8 %all-reduce.6.cloned.1.call-done = bf16[576,128]{1,0:T(8,128)(2,1)} async-done(((bf16[576,128]{1,0:T(8,128)(2,1)}), bf16[576,128]{1,0:T(8,128)(2,1)}) %all-reduce.6.cloned.1.call-update) | async-done | bytes 147472 | tf_op jit(solution)/shard_map/psum | solution.py:357
  525.8 1.6 convert_element_type.192
  527.4 242.0 %all-gather.6.cloned.1.call-done = bf16[4608,4608]{1,0:T(8,128)(2,1)} async-done(((bf16[288,4608]{1,0:T(8,128)(2,1)}), bf16[4608,4608]{1,0:T(8,128)(2,1)}) %all-gather.6.cloned.1.call-update) | async-done | bytes 42467344 | tf_op jit(solution)/shard_map/all_gather | solution.py:371
  769.4 14.3 %reduce_sum.201 = bf16[288,4608]{1,0:T(8,128)(2,1)S(1)} reduce(bf16[16,288,4608]{2,1,0:T(8,128)(2,1)} %bitcast.230, bf16[]{:T(256)} %constant.84.clone.1), dimensions={0}, to_apply=%region_29.30 | reduce | flops 19906560 | bytes 45121536 | tf_op jit(solution)/shard_map/reduce_sum | solution.py:371
  784.0 10.4 %psum.133 = f32[288]{0:T(512)S(1)} all-reduce(f32[288]{0:T(512)S(1)} %fusion.60), channel_id=1, replica_groups=mesh['dp_0'=4,'dp_1'=2,'tensor_0'=4,'tensor_1'=4] {'tensor_0'}, use_global_device_ids=true, to_apply=%region_31.32 | all-reduce | flops 288 | bytes 2304 | tf_op jit(solution)/shard_map/psum | solution.py:23
  794.4 8.6 %psum.134 = f32[288]{0:T(512)S(1)} all-reduce(f32[288]{0:T(512)S(1)} %psum.133), channel_id=1, replica_groups=mesh['dp_0'=4,'dp_1'=2,'tensor_0'=4,'tensor_1'=4] {'tensor_1'}, use_global_device_ids=true, to_apply=%region_32.33 | all-reduce | flops 288 | bytes 2304 | tf_op jit(solution)/shard_map/psum | solution.py:23
  (153 shorter events, 29.2 us)
Async XLA Ops:
  7.2 152.8 %copy-start = (bf16[64,256]{1,0:T(8,128)(2,1)S(1)}, bf16[64,256]{1,0:T(8,128)(2,1)}, u32[]{:S(2)}) copy-start(bf16[64,256]{1,0:T(8,128)(2,1)} %param.28) | copy-start | bytes 98308
  7.2 6.2 copy-start.3
  7.2 6.2 copy-start.8
  7.2 139.3 %all-gather.4.cloned.1.call-start = ((), (), s32[]{:S(2)}) async-start(), calls=%async_computation.8 | async-start | bytes 9289728 | tf_op jit(solution)/shard_map/all_gather | solution.py:62
  36.6 44.0 %copy-start.28 = (f32[288]{0:T(512)}, f32[288]{0:T(512)S(1)}, u32[]{:S(2)}) copy-start(f32[288]{0:T(512)S(1)} %get-tuple-element.43) | copy-start | bytes 3460
  82.7 4.7 copy-start.33
  82.7 45.8 %all-to-all-start = ((bf16[16,288,288]{2,1,0:T(8,128)(2,1)}), bf16[16,288,288]{2,1,0:T(8,128)(2,1)}, u32[]{:S(2)}, u32[]{:S(2)}) async-start(bf16[16,288,288]{2,1,0:T(8,128)(2,1)} %broadcast_in_dim.24), calls=%async_computation | async-start | bytes 7077888 | tf_op jit(solution)/shard_map/all_to_all | solution.py:28
  139.3 33.9 %copy-start.1 = (bf16[288,4608]{1,0:T(8,128)(2,1)}, bf16[288,4608]{1,0:T(8,128)(2,1)S(1)}, u32[]{:S(2)}) copy-start(bf16[288,4608]{1,0:T(8,128)(2,1)S(1)} %reshape.369) | copy-start | bytes 7962628
  154.4 2.1 copy-start.26
  162.4 3.5 copy-start.5
  165.9 2.3 copy-start.7
  168.2 2.2 copy-start.14
  170.3 2.5 copy-start.23
  170.3 2.9 copy-start.25
  171.1 0.9 copy-start.17
  171.1 0.9 copy-start.19
  172.1 0.7 copy-start.9
  172.1 0.7 copy-start.11
  173.2 2.3 copy-start.15
  173.2 2.3 copy-start.31
  175.5 0.6 copy-start.36
  189.2 9.0 %copy-start.21 = (bf16[3,96,2,64]{3,1,2,0:T(8,128)(2,1)S(1)}, bf16[3,96,2,64]{3,1,2,0:T(8,128)(2,1)}, u32[]{:S(2)}) copy-start(bf16[3,96,2,64]{3,1,2,0:T(8,128)(2,1)} %get-tuple-element.28) | copy-start | bytes 221188
  189.2 9.0 %copy-start.22 = (bf16[3,96,2,64]{3,1,2,0:T(8,128)(2,1)S(1)}, bf16[3,96,2,64]{3,1,2,0:T(8,128)(2,1)}, u32[]{:S(2)}) copy-start(bf16[3,96,2,64]{3,1,2,0:T(8,128)(2,1)} %get-tuple-element.29) | copy-start | bytes 221188
  189.2 11.6 %copy-start.6 = (bf16[3,96,4608]{2,1,0:T(8,128)(2,1)S(1)}, bf16[3,96,4608]{2,1,0:T(8,128)(2,1)}, u32[]{:S(2)}) copy-start(bf16[3,96,4608]{2,1,0:T(8,128)(2,1)} %dot_general.122) | copy-start | bytes 7962628
  189.2 52.4 %all-to-all-start.1 = ((bf16[16,288,288]{2,1,0:T(8,128)(2,1)}), bf16[16,288,288]{2,1,0:T(8,128)(2,1)}, u32[]{:S(2)}, u32[]{:S(2)}) async-start(bf16[16,288,288]{2,1,0:T(8,128)(2,1)} %bitcast.232), calls=%async_computation.1 | async-start | bytes 7077888 | tf_op jit(solution)/shard_map/all_to_all | solution.py:52
  241.6 7.0 copy-start.34
  241.6 49.3 %all-to-all-start.3 = ((bf16[16,288,288]{2,1,0:T(8,128)(2,1)}), bf16[16,288,288]{2,1,0:T(8,128)(2,1)}, u32[]{:S(2)}, u32[]{:S(2)}) async-start(bf16[16,288,288]{2,1,0:T(8,128)(2,1)} %bitcast.231), calls=%async_computation.3 | async-start | bytes 7077888 | tf_op jit(solution)/shard_map/all_to_all | solution.py:52
  251.5 60.5 %copy-start.4 = (bf16[288,288]{1,0:T(8,128)(2,1)S(1)}, bf16[288,288]{1,0:T(8,128)(2,1)}, u32[]{:S(2)}) copy-start(bf16[288,288]{1,0:T(8,128)(2,1)} %param.17) | copy-start | bytes 497668
  415.7 3.6 copy-start.16
  415.7 3.6 copy-start.24
  415.7 3.6 copy-start.32
  415.7 3.8 copy-start.10
  415.7 3.8 copy-start.12
  415.7 4.1 copy-start.18
  415.7 4.1 copy-start.20
  416.8 3.3 copy-start.27
  416.8 3.5 copy-start.13
  419.3 1.8 copy-start.2
  423.3 20.8 %all-to-all-start.5 = ((bf16[8,576,128]{2,1,0:T(8,128)(2,1)}), bf16[8,576,128]{2,1,0:T(8,128)(2,1)S(1)}, u32[]{:S(2)}, u32[]{:S(2)}) async-start(bf16[8,576,128]{2,1,0:T(8,128)(2,1)} %bitcast.72), calls=%async_computation.5 | async-start | bytes 2359296 | tf_op jit(solution)/shard_map/all_to_all | solution.py:52
  426.8 98.9 %all-reduce.6.cloned.1.call-start = ((), (), s32[]{:S(2)}) async-start(), calls=%async_computation.9 | async-start | bytes 294912 | tf_op jit(solution)/shard_map/psum | solution.py:357
  445.0 324.4 %all-gather.6.cloned.1.call-start = ((), (), s32[]{:S(2)}) async-start(), calls=%async_computation.10 | async-start | bytes 45121536 | tf_op jit(solution)/shard_map/all_gather | solution.py:371
  450.3 14.5 %copy-start.35 = (f32[12,1]{0,1:T(1,128)S(1)}, f32[12,1]{0,1:T(1,128)}, u32[]{:S(2)}) copy-start(f32[12,1]{0,1:T(1,128)} %get-tuple-element.21) | copy-start | bytes 148
  451.3 9.4 %all-to-all-start.7 = ((bf16[8,64,128]{2,1,0:T(8,128)(2,1)}), bf16[8,64,128]{2,1,0:T(8,128)(2,1)S(1)}, u32[]{:S(2)}, u32[]{:S(2)}) async-start(bf16[8,64,128]{2,1,0:T(8,128)(2,1)} %broadcast_in_dim.35), calls=%async_computation.7 | async-start | bytes 262144 | tf_op jit(solution)/shard_map/all_to_all | solution.py:28
  461.4 10.9 %all-to-all-start.6 = ((bf16[8,64,256]{2,1,0:T(8,128)(2,1)}), bf16[8,64,256]{2,1,0:T(8,128)(2,1)S(1)}, u32[]{:S(2)}, u32[]{:S(2)}) async-start(bf16[8,64,256]{2,1,0:T(8,128)(2,1)} %broadcast_in_dim.34), calls=%async_computation.6 | async-start | bytes 524288 | tf_op jit(solution)/shard_map/all_to_all | solution.py:28
  769.4 33.6 %copy-start.29 = (f32[288]{0:T(512)S(1)}, f32[288]{0:T(512)}, u32[]{:S(2)}) copy-start(f32[288]{0:T(512)} %copy-done.28) | copy-start | bytes 3460
  769.4 33.6 %copy-start.30 = (f32[288]{0:T(512)S(1)}, f32[288]{0:T(512)}, u32[]{:S(2)}) copy-start(f32[288]{0:T(512)} %get-tuple-element.42) | copy-start | bytes 3460
Sparse Core Ops, SparseCore 0:
  12.7 51.5 all-gather.3
  445.1 80.6 all-reduce.5
  528.0 241.3 all-gather.5
